TPU v7x, 32 devices: a whole 2x2x4 slice. The times are simulated.
32 devices in a mesh: groups: 2 (over x), tensor: 16 (over z, y, core).
Axes of the slice: x: 2, y: 2, z: 4, core: 2. Of those that a mesh axis runs over, the one named last changes fastest.
Arguments:
- video_state: float32 [128, 4096], P(('groups', 'tensor')), parts along dimension 0, may hold values from -54 to 54
- audio_state: float32 [128, 2048], P(('groups', 'tensor')), parts along dimension 0, may hold values from -54 to 54
- video_modulation: float32 [12, 4096], P('groups'), parts along dimension 0, may hold values from -3 to 3
- audio_modulation: float32 [12, 2048], P('groups'), parts along dimension 0, may hold values from -3 to 3
- video_query: bfloat16 [4096, 2048], P(None, 'tensor'), may hold values from -0.09375 to 0.09375
- audio_keyval: bfloat16 [2048, 2, 2048], P(None, None, 'tensor'), may hold values from -0.125 to 0.125
- video_output: bfloat16 [2048, 4096], P('tensor'), may hold values from -0.125 to 0.125
- audio_query: bfloat16 [2048, 2048], P(None, 'tensor'), may hold values from -0.125 to 0.125
- video_keyval: bfloat16 [4096, 2, 2048], P(None, None, 'tensor'), may hold values from -0.09375 to 0.09375
- audio_output: bfloat16 [2048, 2048], P('tensor'), may hold values from -0.125 to 0.125
- video_expand: bfloat16 [4096, 16384], P(None, 'tensor'), may hold values from -0.09375 to 0.09375
- video_shrink: bfloat16 [16384, 4096], P('tensor'), may hold values from -0.046875 to 0.046875
- audio_expand: bfloat16 [2048, 8192], P(None, 'tensor'), may hold values from -0.125 to 0.125
- audio_shrink: bfloat16 [8192, 2048], P('tensor'), may hold values from -0.0625 to 0.0625
Outputs:
- video_next: float32 [128, 4096], P(('groups', 'tensor')), parts along dimension 0
- audio_next: float32 [128, 2048], P(('groups', 'tensor')), parts along dimension 0
There are 2 independent parts, one for each index of `groups`. A program takes and returns all parts, laid end to end along the dimension named above; an argument that names none is the same for every part. Nothing has to cross between parts.
All inputs are finite; a program needn't handle non-finite values.
Results may differ from a plain program's by a relative error of at most 0.0029.
Values may be sent and summed in bfloat16 or wider, within the bound.
A program may use at most 64 MiB of HBM per device.

v0:
```python
import jax
import jax.numpy as jnp
from jax import lax
from jax.sharding import PartitionSpec as P

HEAD_DIM = 64


epsilon = 1e-06


def partner(block, axis, distance):
    count = lax.axis_size(axis)
    route = []
    for low in range(count):
        high = low | 1 << distance
        if high != low and high < count:
            route += [(low, high), (high, low)]
    return lax.ppermute(block, axis, route)


def modulate(states, modulation, first):
    normed = states * lax.rsqrt(jnp.mean(states * states, axis=-1, keepdims=True) + epsilon)
    return (normed * (1.0 + modulation[first + 1]) + modulation[first]).astype(jnp.bfloat16)


def head_normalize(tensor):
    values = tensor.astype(jnp.float32)
    return (values * lax.rsqrt(jnp.mean(values * values, axis=-1, keepdims=True) + epsilon)).astype(
        jnp.bfloat16
    )


def softmax_weights(scores):
    expo = jnp.exp(scores)
    return (expo / jnp.sum(expo, axis=-1, keepdims=True)).astype(jnp.bfloat16)


def local_heads(queries, key_part, value_part):
    query_count, width = queries.shape
    source_count = key_part.shape[0]
    head_count = width // HEAD_DIM
    query_hat = head_normalize(queries.reshape(query_count, head_count, HEAD_DIM))
    key_hat = head_normalize(key_part.reshape(source_count, head_count, HEAD_DIM))
    scores = jnp.einsum(
        "qhd,khd->hqk", query_hat, key_hat, preferred_element_type=jnp.float32
    ) * HEAD_DIM ** (-0.5)
    weights = softmax_weights(scores)
    values = value_part.reshape(source_count, head_count, HEAD_DIM)
    mixed = jnp.einsum("hqk,khd->qhd", weights, values, preferred_element_type=jnp.float32)
    return mixed.astype(jnp.bfloat16).reshape(query_count, width)


def project_attend(query_rows, source_rows, query_weight, keyval_weight):
    width = query_weight.shape[1]
    queries = jnp.dot(query_rows, query_weight, preferred_element_type=jnp.float32).astype(
        jnp.bfloat16
    )
    flat_weight = keyval_weight.reshape(keyval_weight.shape[0], 2 * width)
    keyvals = jnp.dot(source_rows, flat_weight, preferred_element_type=jnp.float32).astype(
        jnp.bfloat16
    )
    key_part = keyvals[:, :width]
    value_part = keyvals[:, width:]
    if width >= HEAD_DIM:
        return local_heads(queries, key_part, value_part)
    query_float = queries.astype(jnp.float32)
    key_float = key_part.astype(jnp.float32)
    query_square = jnp.sum(query_float * query_float, axis=1, keepdims=True)
    key_square = jnp.sum(key_float * key_float, axis=1, keepdims=True)
    other_query, other_key = partner((query_square, key_square), "tensor", 0)
    query_hat = (query_float * lax.rsqrt((query_square + other_query) / HEAD_DIM + epsilon)).astype(
        jnp.bfloat16
    )
    key_hat = (key_float * lax.rsqrt((key_square + other_key) / HEAD_DIM + epsilon)).astype(
        jnp.bfloat16
    )
    partial_scores = jnp.einsum("qd,kd->qk", query_hat, key_hat, preferred_element_type=jnp.float32)
    other_scores = partner(partial_scores, "tensor", 0)
    scores = (partial_scores + other_scores) * HEAD_DIM ** (-0.5)
    weights = softmax_weights(scores)
    return jnp.dot(weights, value_part, preferred_element_type=jnp.float32).astype(jnp.bfloat16)


def output_rows(mixed, weight):
    return jnp.dot(mixed, weight, preferred_element_type=jnp.float32)


def feed_rows(inputs, expand, shrink):
    hidden = jnp.dot(inputs, expand, preferred_element_type=jnp.float32)
    hidden = jax.nn.gelu(hidden, approximate=True).astype(jnp.bfloat16)
    return jnp.dot(hidden, shrink, preferred_element_type=jnp.float32)


def on_device(
    video_state,
    audio_state,
    video_modulation,
    audio_modulation,
    video_query,
    audio_keyval,
    video_output,
    audio_query,
    video_keyval,
    audio_output,
    video_expand,
    video_shrink,
    audio_expand,
    audio_shrink,
):
    video_count = video_state.shape[0]
    audio_own = modulate(audio_state, audio_modulation, 0)
    video_whole = lax.all_gather(video_state, "tensor", axis=0, tiled=True)
    video_normed = modulate(video_whole, video_modulation, 0)
    audio_normed = lax.all_gather(audio_own, "tensor", axis=0, tiled=True)
    video_mixed = project_attend(video_normed, audio_normed, video_query, audio_keyval)
    audio_mixed = project_attend(audio_normed, video_normed, audio_query, video_keyval)
    audio_term = lax.psum_scatter(
        output_rows(audio_mixed, audio_output), "tensor", scatter_dimension=0, tiled=True
    )
    audio_mid = audio_state + audio_modulation[2] * audio_term
    audio_inner_own = modulate(audio_mid, audio_modulation, 3)
    partial_term = jnp.dot(video_mixed, video_output, preferred_element_type=jnp.float32)
    full_term = lax.psum(partial_term, "tensor")
    video_mid_whole = video_whole + video_modulation[2] * full_term
    video_inner = modulate(video_mid_whole, video_modulation, 3)
    first_row = lax.axis_index("tensor") * video_count
    video_mid = lax.dynamic_slice_in_dim(video_mid_whole, first_row, video_count, 0)
    audio_inner = lax.all_gather(audio_inner_own, "tensor", axis=0, tiled=True)
    video_feed = lax.psum_scatter(
        feed_rows(video_inner, video_expand, video_shrink),
        "tensor",
        scatter_dimension=0,
        tiled=True,
    )
    audio_feed = lax.psum_scatter(
        feed_rows(audio_inner, audio_expand, audio_shrink),
        "tensor",
        scatter_dimension=0,
        tiled=True,
    )
    video_next = video_mid + video_modulation[5] * video_feed
    audio_next = audio_mid + audio_modulation[5] * audio_feed
    return (video_next, audio_next)


def solution(mesh):
    placed = (
        P(("groups", "tensor"), None),
        P(("groups", "tensor"), None),
        P("groups", None),
        P("groups", None),
        P(None, "tensor"),
        P(None, None, "tensor"),
        P("tensor", None),
        P(None, "tensor"),
        P(None, None, "tensor"),
        P("tensor", None),
        P(None, "tensor"),
        P("tensor", None),
        P(None, "tensor"),
        P("tensor", None),
    )
    return jax.shard_map(
        on_device,
        mesh=mesh,
        in_specs=placed,
        out_specs=(P(("groups", "tensor"), None), P(("groups", "tensor"), None)),
        check_vma=False,
    )
```

profile of v0, /device:TPU:0, one launch (start us, length us, event | category | flops | bytes accessed | tf_op | source)
XLA Modules:
  0.0 302.8 jit_solution(14228679446785322309)
XLA Ops:
  7.2 0.0 copy-start
  7.2 0.0 copy-start.3
  7.2 0.0 all-gather.5.cloned.1.call-start
  7.2 0.7 all-gather.5.cloned.1.call-update
  7.9 0.0 all-reduce.10.cloned.1.call-start
  8.0 1.8 fusion.80
  9.7 0.9 multiply_reduce_fusion.7
  10.6 0.8 fusion.54
  11.5 24.0 %all-gather.1 = bf16[16,4,2048]{2,1,0:T(4,128)(2,1)S(1)} all-gather(bf16[1,4,2048]{2,1,0:T(4,128)(2,1)S(1)} %fusion.54), channel_id=1, replica_groups=mesh['groups'=2,'tensor'=16] {'tensor'}, dimensions={0}, use_global_device_ids=true | all-gather | bytes 278528 | tf_op jit(solution)/shard_map/all_gather | solution.py:115
  35.5 0.1 reshape.113
  35.5 1.3 fusion.9
  36.8 0.1 reshape.108
  36.9 1.5 convolution_convert_fusion.2
  38.5 0.1 reshape.107
  38.6 0.7 copy.50
  39.3 0.1 multiply_reduce_fusion.3
  39.4 0.1 multiply_reduce_fusion.4
  39.6 0.0 copy-done.3
  39.6 0.7 fusion.79
  40.3 10.6 %all-gather.5.cloned.1.call-done = f32[16,4,4096]{2,1,0:T(4,128)} async-done(((f32[1,4,4096]{2,1,0:T(4,128)}), f32[16,4,4096]{2,1,0:T(4,128)}) %all-gather.5.cloned.1.call-update) | async-done | bytes 1048592 | tf_op jit(solution)/shard_map/all_gather | solution.py:113
  50.9 1.6 reshape.111
  52.5 0.2 multiply_reduce_fusion.1
  52.7 2.1 fusion.5
  54.9 0.0 copy-done.4
  54.9 0.0 copy-done.5
  54.9 0.1 reshape.109
  55.0 0.1 multiply_reduce_fusion.2
  55.2 0.7 copy.51
  55.9 1.6 fusion.8
  57.5 0.1 reshape.106
  57.6 0.1 multiply_reduce_fusion.5
  57.8 0.2 multiply_convert_fusion
  58.0 0.1 fusion.3
  58.1 0.9 convolution_convert_fusion
  59.0 2.1 fusion.84
  61.2 0.2 multiply_convert_fusion.2
  61.4 0.0 copy-start.13
  61.4 0.0 copy-start.2
  61.4 0.0 copy-start.12
  61.4 0.1 fusion.4
  61.5 0.0 copy-start.10
  61.6 0.0 copy-start.11
  61.6 0.9 convolution_convert_fusion.1
  62.5 2.6 fusion.83
  65.1 0.0 all-reduce.10.cloned.1.call-update
  65.1 0.0 all-reduce.8.cloned.1.call-start
  65.2 0.0 copy-done.13
  65.2 0.6 dynamic-slice
  66.4 93.9 %all-reduce.10.cloned.1.call-done = (f32[64,4096]{1,0:T(8,128)}, f32[64,2048]{1,0:T(8,128)}) async-done(((f32[64,4096]{1,0:T(8,128)}, f32[64,2048]{1,0:T(8,128)}), (f32[64,4096]{1,0:T(8,128)}, f32[64,2048]{1,0:T(8,128)})) %all-reduce.10.cloned.1.call-update) | async-done | bytes 1572880 | tf_op jit(solution)/shard_map/psum | solution.py:124
  160.3 0.0 copy-done.2
  160.3 0.0 copy-done.12
  160.3 1.0 multiply_reduce_fusion.6
  161.3 0.0 copy-done.10
  161.3 0.1 fusion.55
  161.4 21.4 %all-gather.2 = bf16[16,4,2048]{2,1,0:T(4,128)(2,1)} all-gather(bf16[1,4,2048]{2,1,0:T(4,128)(2,1)S(1)} %fusion.55), channel_id=1, replica_groups=mesh['groups'=2,'tensor'=16] {'tensor'}, dimensions={0}, use_global_device_ids=true | all-gather | bytes 278528 | tf_op jit(solution)/shard_map/all_gather | solution.py:129
  182.8 1.0 reshape.115
  183.8 2.5 multiply_reduce_fusion
  186.4 3.4 %fusion.37 = f32[64,2048]{1,0:T(8,128)} fusion(bf16[512,2048]{1,0:T(8,128)(2,1)S(1)} %copy-done, bf16[64,2048]{1,0:T(8,128)(2,1)S(1)} %reshape.115, bf16[2048,512]{1,0:T(8,128)(2,1)} %param.26), kind=kOutput, calls=%fused_computation.49 | convolution fusion | flops 268730368 | bytes 4980736 | tf_op jit(solution)/shard_map/dot_general | solution.py:92
  189.8 0.0 copy-done.7
  189.8 9.9 %fusion.24 = f32[64,4096]{1,0:T(8,128)} fusion(bf16[1024,4096]{1,0:T(8,128)(2,1)} %param.25, bf16[4096,1024]{1,0:T(8,128)(2,1)} %param.24, f32[64,4096]{1,0:T(8,128)S(1)} %copy-done.1, f32[4096]{0:T(1024)S(1)} %bitcast.60, f32[4096]{0:T(1024)S(1)} %bitcast.61, f32[64]{0:T(128)S(1)} %add_rsqrt_fusion.5), kind=kOutput, calls=%fused_computation.35 | convolution fusion | flops 1075380224 | bytes 18907392 | tf_op jit(solution)/shard_map/dot_general | solution.py:92
  199.8 0.0 all-reduce.8.cloned.1.call-update
  199.8 93.4 %all-reduce.8.cloned.1.call-done = (f32[64,4096]{1,0:T(8,128)}, f32[64,2048]{1,0:T(8,128)}) async-done(((f32[64,4096]{1,0:T(8,128)}, f32[64,2048]{1,0:T(8,128)}), (f32[64,4096]{1,0:T(8,128)}, f32[64,2048]{1,0:T(8,128)})) %all-reduce.8.cloned.1.call-update) | async-done | bytes 1572880
  293.2 1.5 fusion.44
  294.7 1.6 fusion.39
  (23 shorter events, 0.1 us)
Async XLA Ops:
  7.2 179.2 %copy-start = (bf16[512,2048]{1,0:T(8,128)(2,1)S(1)}, bf16[512,2048]{1,0:T(8,128)(2,1)}, u32[]{:S(2)}) copy-start(bf16[512,2048]{1,0:T(8,128)(2,1)} %param.27) | copy-start | bytes 6291460
  7.2 32.4 %copy-start.3 = (f32[6,4096]{1,0:T(8,128)S(1)}, f32[6,4096]{1,0:T(8,128)}, u32[]{:S(2)}) copy-start(f32[6,4096]{1,0:T(8,128)} %param.16) | copy-start | bytes 294916
  7.2 43.8 %all-gather.5.cloned.1.call-start = ((), (), s32[]{:S(2)}) async-start(), calls=%async_computation | async-start | bytes 1114112 | tf_op jit(solution)/shard_map/all_gather | solution.py:113
  7.9 152.4 %all-reduce.10.cloned.1.call-start = ((), (), s32[]{:S(2)}) async-start(), calls=%async_computation.2 | async-start | bytes 3145728 | tf_op jit(solution)/shard_map/psum | solution.py:124
  40.3 14.5 %copy-start.4 = (f32[1,4096]{1,0:T(1,128)}, f32[1,4096]{1,0:T(1,128)S(1)}, u32[]{:S(2)}) copy-start(f32[1,4096]{1,0:T(1,128)S(1)} %get-tuple-element.11) | copy-start | bytes 49156
  40.3 14.6 %copy-start.5 = (f32[1,4096]{1,0:T(1,128)}, f32[1,4096]{1,0:T(1,128)S(1)}, u32[]{:S(2)}) copy-start(f32[1,4096]{1,0:T(1,128)S(1)} %get-tuple-element.12) | copy-start | bytes 49156
  61.4 3.8 %copy-start.13 = (u32[32]{0:T(128)S(1)}, u32[32]{0:T(128)}, u32[]{:S(2)}) copy-start(u32[32]{0:T(128)} %constant.50) | copy-start | bytes 388
  61.4 99.0 %copy-start.2 = (f32[4,2048]{1,0:T(4,128)S(1)}, f32[4,2048]{1,0:T(4,128)}, u32[]{:S(2)}) copy-start(f32[4,2048]{1,0:T(4,128)} %param.15) | copy-start | bytes 98308
  61.4 98.9 %copy-start.12 = (f32[1,2048]{1,0:T(1,128)S(1)}, f32[1,2048]{1,0:T(1,128)}, u32[]{:S(2)}) copy-start(f32[1,2048]{1,0:T(1,128)} %get-tuple-element.17) | copy-start | bytes 24580
  61.5 99.8 %copy-start.10 = (f32[1,2048]{1,0:T(1,128)S(1)}, f32[1,2048]{1,0:T(1,128)}, u32[]{:S(2)}) copy-start(f32[1,2048]{1,0:T(1,128)} %get-tuple-element.20) | copy-start | bytes 24580
  61.6 99.8 %copy-start.11 = (f32[1,2048]{1,0:T(1,128)S(1)}, f32[1,2048]{1,0:T(1,128)}, u32[]{:S(2)}) copy-start(f32[1,2048]{1,0:T(1,128)} %get-tuple-element.21) | copy-start | bytes 24580
  65.1 228.1 %all-reduce.8.cloned.1.call-start = ((), (), s32[]{:S(2)}) async-start(), calls=%async_computation.1 | async-start | bytes 3145728
  186.3 3.4 %copy-start.1 = (f32[64,4096]{1,0:T(8,128)S(1)}, f32[64,4096]{1,0:T(8,128)}, u32[]{:S(2)}) copy-start(f32[64,4096]{1,0:T(8,128)} %get-tuple-element.9) | copy-start | bytes 3145732
  186.3 3.4 %copy-start.7 = (f32[1,4096]{1,0:T(1,128)S(1)}, f32[1,4096]{1,0:T(1,128)}, u32[]{:S(2)}) copy-start(f32[1,4096]{1,0:T(1,128)} %get-tuple-element.14) | copy-start | bytes 49156
  186.3 3.4 %copy-start.8 = (f32[1,4096]{1,0:T(1,128)S(1)}, f32[1,4096]{1,0:T(1,128)}, u32[]{:S(2)}) copy-start(f32[1,4096]{1,0:T(1,128)} %get-tuple-element.15) | copy-start | bytes 49156
  189.8 103.4 %copy-start.9 = (f32[1,2048]{1,0:T(1,128)S(1)}, f32[1,2048]{1,0:T(1,128)}, u32[]{:S(2)}) copy-start(f32[1,2048]{1,0:T(1,128)} %get-tuple-element.16) | copy-start | bytes 24580
  189.8 104.9 %copy-start.6 = (f32[1,4096]{1,0:T(1,128)S(1)}, f32[1,4096]{1,0:T(1,128)}, u32[]{:S(2)}) copy-start(f32[1,4096]{1,0:T(1,128)} %get-tuple-element.10) | copy-start | bytes 49156
Sparse Core Ops, SparseCore 0:
  10.2 40.7 all-gather.4
  65.2 95.0 all-reduce.9
  199.9 93.2 all-reduce.7
where the time goes:
time: 304 us; the launch traced here: 303 us
  waiting for transfers between devices  199 us (65%)
  blocking collectives  45.4 us (15%)
  matrix products  26.7 us (9%)
  between operations  14.8 us (5%)
  other arithmetic  12 us (4%)
  local copies, waits for them, and re-layouts  5.14 us (2%)
    unnamed x4, waiting for transfers between devices  94.1 us
    psum x1, waiting for transfers between devices, on_device(): full_term = lax.psum(partial_term, 'tensor')  93.9 us
    all_gather x1, blocking collectives, on_device(): audio_normed = lax.all_gather(audio_own, 'tensor', axis=0, tiled=True)  24 us
    all_gather x1, blocking collectives, on_device(): audio_inner = lax.all_gather(audio_inner_own, 'tensor', axis=0, tiled=True)  21.4 us
    dot_general x2, matrix products, feed_rows(): return jnp.dot(hidden, shrink, preferred_element_type=jnp.float32)  13.4 us
    all_gather x1, waiting for transfers between devices, on_device(): video_whole = lax.all_gather(video_state, 'tensor', axis=0, tiled=True)  10.6 us
  transfers between devices with their start and end apart: 3, of which 3 were waited for; matrix products, arithmetic and copies ran while one was open for 3% of the time, Pallas kernels for 0%

commit v1 on v0

--- a/solution.py
+++ b/solution.py
@@ -1,6 +1,10 @@
+import functools
+
 import jax
 import jax.numpy as jnp
 from jax import lax
+from jax.experimental import pallas as pl
+from jax.experimental.pallas import tpu as pltpu
 from jax.sharding import PartitionSpec as P
 
 HEAD_DIM = 64
@@ -144,6 +148,408 @@
     return (video_next, audio_next)
 
 
+VMEM_BYTES = 66_000_000
+WEIGHT_BYTES = 40 << 20
+
+
+def matmul_to(lhs_ref, weight_ref, tile, emit):
+    def body(i, carry):
+        columns = pl.ds(pl.multiple_of(i * tile, tile), tile)
+        emit(
+            columns,
+            jnp.dot(lhs_ref[...], weight_ref[:, columns], preferred_element_type=jnp.float32),
+        )
+        return carry
+
+    lax.fori_loop(0, weight_ref.shape[1] // tile, body, 0)
+
+
+class Stream:
+    names = ("own", "slots", "wide", "whole", "other", "paired", "sums", "terms", "total")
+
+    @staticmethod
+    def scratch(count, rows, width):
+        chips = count // 2
+        return [
+            pltpu.VMEM((rows, width), jnp.bfloat16),
+            pltpu.VMEM((count, rows, width), jnp.bfloat16),
+            pltpu.VMEM((chips, 2 * rows, width), jnp.float32),
+            pltpu.VMEM((count * rows, width), jnp.bfloat16),
+            pltpu.VMEM((chips, rows, width), jnp.bfloat16),
+            pltpu.VMEM((chips, rows, width), jnp.bfloat16),
+            pltpu.VMEM((chips, rows, width), jnp.bfloat16),
+            pltpu.VMEM((chips, rows, width), jnp.bfloat16),
+            pltpu.VMEM((rows, width), jnp.float32),
+            pltpu.SemaphoreType.DMA((2 * chips,)),
+            pltpu.SemaphoreType.DMA((count,)),
+            pltpu.SemaphoreType.DMA((chips + 1,)),
+            pltpu.SemaphoreType.DMA((chips + 1,)),
+        ]
+
+    def __init__(self, refs, count):
+        for name, ref in zip(self.names, refs):
+            setattr(self, name, ref)
+        self.gather_send, self.gather_recv, self.scatter_send, self.scatter_recv = refs[len(self.names):]
+        self.count, self.chips = count, count // 2
+        self.rows = self.own.shape[0]
+        self.me = lax.axis_index("tensor")
+        self.chip, self.core = self.me // 2, self.me % 2
+        self.mate = self.chip * 2 + (1 - self.core)
+
+    def distant(self, step):
+        return lax.rem(self.chip + step, self.chips)
+
+    def to_mate(self, slot, source, send):
+        return pltpu.make_async_remote_copy(
+            src_ref=source,
+            dst_ref=self.slots.at[slot],
+            send_sem=self.gather_send.at[send],
+            recv_sem=self.gather_recv.at[slot],
+            device_id={"tensor": self.mate},
+            device_id_type=pl.DeviceIdType.MESH,
+        )
+
+    def to_chip(self, step):
+        return pltpu.make_async_remote_copy(
+            src_ref=self.own,
+            dst_ref=self.slots.at[self.me],
+            send_sem=self.gather_send.at[step],
+            recv_sem=self.gather_recv.at[self.me],
+            device_id={"tensor": self.distant(step) * 2 + self.core},
+            device_id_type=pl.DeviceIdType.MESH,
+        )
+
+    def keep(self):
+        return pltpu.make_async_copy(self.own, self.slots.at[self.me], self.gather_recv.at[self.me])
+
+    def gather_start(self):
+        for step in range(self.chips - 1, 0, -1):
+            self.to_chip(step).start()
+        self.to_mate(self.me, self.own, 0).start()
+        self.keep().start()
+
+    def arrived(self, slot):
+        pltpu.make_async_copy(self.slots.at[slot], self.slots.at[slot], self.gather_recv.at[slot]).wait()
+
+    def gather_forward(self):
+        for step in range(1, self.chips):
+            slot = self.distant(step) * 2 + self.core
+            self.arrived(slot)
+            self.to_mate(slot, self.slots.at[slot], self.chips + step).start()
+
+    def gather_finish(self):
+        self.keep().wait()
+        for step in range(self.chips):
+            self.arrived(self.distant(step) * 2 + 1 - self.core)
+
+        def widen(chip, carry):
+            self.wide[chip, : self.rows, :] = self.slots[2 * chip].astype(jnp.float32)
+            self.wide[chip, self.rows :, :] = self.slots[2 * chip + 1].astype(jnp.float32)
+            return carry
+
+        lax.fori_loop(0, self.chips, widen, 0)
+        self.whole[...] = self.wide[...].reshape(self.whole.shape).astype(jnp.bfloat16)
+
+    def gather_drain(self):
+        for step in range(1, self.chips):
+            slot = self.distant(step) * 2 + self.core
+            self.to_chip(step).wait_send()
+            self.to_mate(slot, self.slots.at[slot], self.chips + step).wait_send()
+        self.to_mate(self.me, self.own, 0).wait_send()
+
+    def emit(self, columns, product):
+        self.wide[:, :, columns] = product.reshape(self.chips, 2 * self.rows, product.shape[1])
+
+    def swap(self):
+        return pltpu.make_async_remote_copy(
+            src_ref=self.other,
+            dst_ref=self.paired,
+            send_sem=self.scatter_send.at[self.chips],
+            recv_sem=self.scatter_recv.at[self.chips],
+            device_id={"tensor": self.mate},
+            device_id_type=pl.DeviceIdType.MESH,
+        )
+
+    def halves(self, chip):
+        rows = self.wide[chip]
+        low, high = rows[: self.rows], rows[self.rows :]
+        first = self.core == 0
+        return jnp.where(first, low, high), jnp.where(first, high, low)
+
+    def scatter_start(self):
+        def body(chip, carry):
+            self.other[chip] = self.halves(chip)[1].astype(jnp.bfloat16)
+            return carry
+
+        lax.fori_loop(0, self.chips, body, 0)
+        self.swap().start()
+
+    def term(self, step):
+        goal = self.distant(step)
+        return pltpu.make_async_remote_copy(
+            src_ref=self.sums.at[goal],
+            dst_ref=self.terms.at[self.chip],
+            send_sem=self.scatter_send.at[step],
+            recv_sem=self.scatter_recv.at[self.chip],
+            device_id={"tensor": goal * 2 + self.core},
+            device_id_type=pl.DeviceIdType.MESH,
+        )
+
+    def scatter_send_on(self):
+        self.swap().wait()
+        for step in range(1, self.chips):
+            goal = self.distant(step)
+            self.sums[goal] = (
+                self.halves(goal)[0] + self.paired[goal].astype(jnp.float32)
+            ).astype(jnp.bfloat16)
+            self.term(step).start()
+        self.total[...] = self.halves(self.chip)[0] + self.paired[self.chip].astype(jnp.float32)
+
+    def scatter_finish(self):
+        for step in range(1, self.chips):
+            source = self.distant(step)
+            pltpu.make_async_copy(
+                self.terms.at[source], self.terms.at[source], self.scatter_recv.at[source]
+            ).wait()
+            self.total[...] += self.terms[source].astype(jnp.float32)
+        for step in range(1, self.chips):
+            self.term(step).wait_send()
+        return self.total[...]
+
+
+def split_pairs(pairs_ref, wide_ref, even_ref, odd_ref, rows):
+    def body(i, carry):
+        start = pl.multiple_of(i * rows, rows)
+        wide_ref[...] = pairs_ref[pl.ds(pl.multiple_of(i * 2 * rows, 2 * rows), 2 * rows), :].astype(
+            jnp.float32
+        )
+        even_ref[pl.ds(start, rows), :] = wide_ref[pl.ds(0, rows, stride=2), :].astype(jnp.bfloat16)
+        odd_ref[pl.ds(start, rows), :] = wide_ref[pl.ds(1, rows, stride=2), :].astype(jnp.bfloat16)
+        return carry
+
+    lax.fori_loop(0, even_ref.shape[0] // rows, body, 0)
+
+
+def segment_normalize(tensor):
+    values = tensor.astype(jnp.float32)
+    squares = values * values
+    head_of = lax.broadcasted_iota(jnp.int32, values.shape, 1) // HEAD_DIM
+    scale = jnp.zeros_like(values)
+    for head in range(values.shape[1] // HEAD_DIM):
+        mine = head_of == head
+        mean = jnp.sum(jnp.where(mine, squares, 0.0), axis=-1, keepdims=True) / HEAD_DIM
+        scale = jnp.where(mine, lax.rsqrt(mean + epsilon), scale)
+    return values * scale
+
+
+def attend(queries, keys, values):
+    query_hat = segment_normalize(queries)
+    key_hat = segment_normalize(keys).astype(jnp.bfloat16)
+    head_of = lax.broadcasted_iota(jnp.int32, query_hat.shape, 1) // HEAD_DIM
+    mixed = jnp.zeros(query_hat.shape, jnp.float32)
+    for head in range(query_hat.shape[1] // HEAD_DIM):
+        mine = head_of == head
+        own = jnp.where(mine, query_hat, 0.0).astype(jnp.bfloat16)
+        scores = lax.dot_general(
+            own, key_hat, (((1,), (1,)), ((), ())), preferred_element_type=jnp.float32
+        ) * HEAD_DIM ** (-0.5)
+        weights = softmax_weights(scores)
+        mixed = jnp.where(mine, jnp.dot(weights, values, preferred_element_type=jnp.float32), mixed)
+    return mixed.astype(jnp.bfloat16)
+
+
+def modulate_rows(states, modulation_ref, first):
+    normed = states * lax.rsqrt(jnp.mean(states * states, axis=-1, keepdims=True) + epsilon)
+    return (
+        normed * (1.0 + modulation_ref[first + 1 : first + 2, :]) + modulation_ref[first : first + 1, :]
+    ).astype(jnp.bfloat16)
+
+
+def project(rows_ref, weight_ref):
+    return jnp.dot(rows_ref[...], weight_ref[...], preferred_element_type=jnp.float32).astype(jnp.bfloat16)
+
+
+def block_kernel(count, video_width, audio_width, *refs):
+    video_state, audio_state, video_mod, audio_mod = refs[:4]
+    weights_hbm = refs[4:14]
+    video_out, audio_out = refs[14:16]
+    weights = refs[16:26]
+    rest = refs[26:]
+    size = 13
+    video1, audio1, video2, audio2 = (
+        Stream(rest[i * size : (i + 1) * size], count) for i in range(4)
+    )
+    (weight_sem, pair_wide, video_key, video_value, audio_key, audio_value,
+     video_mixed, audio_mixed, video_hidden, audio_hidden) = rest[4 * size :]
+    loads = [
+        pltpu.make_async_copy(hbm, vmem, weight_sem.at[i])
+        for i, (hbm, vmem) in enumerate(zip(weights_hbm, weights))
+    ]
+    (audio_query, audio_pairs, video_query, video_pairs, audio_output, video_output,
+     audio_expand, audio_shrink, video_expand, video_shrink) = weights
+    for load in loads:
+        load.start()
+
+    barrier = pltpu.get_barrier_semaphore()
+    for step in range(1, video1.chips):
+        pl.semaphore_signal(
+            barrier,
+            inc=1,
+            device_id={"tensor": video1.distant(step) * 2 + video1.core},
+            device_id_type=pl.DeviceIdType.MESH,
+        )
+    pl.semaphore_signal(
+        barrier, inc=1, device_id={"tensor": video1.mate}, device_id_type=pl.DeviceIdType.MESH
+    )
+    audio1.own[...] = modulate_rows(audio_state[...], audio_mod, 0)
+    video1.own[...] = modulate_rows(video_state[...], video_mod, 0)
+    pl.semaphore_wait(barrier, video1.chips)
+
+    audio1.gather_start()
+    video1.gather_start()
+    loads[1].wait()
+    split_pairs(audio_pairs, pair_wide, audio_key, audio_value, pair_wide.shape[0] // 2)
+    audio1.gather_forward()
+    loads[3].wait()
+    split_pairs(video_pairs, pair_wide, video_key, video_value, pair_wide.shape[0] // 2)
+    audio1.gather_finish()
+    loads[0].wait()
+    audio_queries = project(audio1.whole, audio_query)
+    audio_keys = project(audio1.whole, audio_key)
+    audio_values = project(audio1.whole, audio_value)
+    video1.gather_forward()
+    video1.gather_finish()
+    loads[2].wait()
+    video_keys = project(video1.whole, video_key)
+    video_values = project(video1.whole, video_value)
+    audio_mixed[...] = attend(audio_queries, video_keys, video_values)
+    loads[4].wait()
+    matmul_to(audio_mixed, audio_output, 512, audio1.emit)
+    audio1.scatter_start()
+    video_queries = project(video1.whole, video_query)
+    video_mixed[...] = attend(video_queries, audio_keys, audio_values)
+    audio1.scatter_send_on()
+    loads[5].wait()
+    matmul_to(video_mixed, video_output, 512, video1.emit)
+    video1.scatter_start()
+    audio1.gather_drain()
+    video1.gather_drain()
+    video1.scatter_send_on()
+    audio_mid = audio_state[...] + audio_mod[2:3, :] * audio1.scatter_finish()
+    audio_out[...] = audio_mid
+    audio2.own[...] = modulate_rows(audio_mid, audio_mod, 3)
+    audio2.gather_start()
+    video_mid = video_state[...] + video_mod[2:3, :] * video1.scatter_finish()
+    video_out[...] = video_mid
+    video2.own[...] = modulate_rows(video_mid, video_mod, 3)
+    video2.gather_start()
+    audio2.gather_forward()
+    audio2.gather_finish()
+
+    def keep_hidden(target):
+        def emit(columns, product):
+            target[:, columns] = jax.nn.gelu(product, approximate=True).astype(jnp.bfloat16)
+
+        return emit
+
+    loads[6].wait()
+    matmul_to(audio2.whole, audio_expand, 256, keep_hidden(audio_hidden))
+    loads[7].wait()
+    matmul_to(audio_hidden, audio_shrink, 512, audio2.emit)
+    audio2.scatter_start()
+    video2.gather_forward()
+    audio2.scatter_send_on()
+    video2.gather_finish()
+    loads[8].wait()
+    matmul_to(video2.whole, video_expand, 256, keep_hidden(video_hidden))
+    loads[9].wait()
+    matmul_to(video_hidden, video_shrink, 512, video2.emit)
+    video2.scatter_start()
+    audio_out[...] += audio_mod[5:6, :] * audio2.scatter_finish()
+    audio2.gather_drain()
+    video2.gather_drain()
+    video2.scatter_send_on()
+    video_out[...] += video_mod[5:6, :] * video2.scatter_finish()
+
+
+def fused_block(
+    video_state,
+    audio_state,
+    video_modulation,
+    audio_modulation,
+    video_query,
+    audio_keyval,
+    video_output,
+    audio_query,
+    video_keyval,
+    audio_output,
+    video_expand,
+    video_shrink,
+    audio_expand,
+    audio_shrink,
+):
+    count = lax.axis_size("tensor")
+    rows, video_width = video_state.shape
+    audio_width = audio_state.shape[1]
+    width = video_query.shape[1]
+    tokens = count * rows
+    weights = (
+        audio_query,
+        audio_keyval.reshape(-1, width),
+        video_query,
+        video_keyval.reshape(-1, width),
+        audio_output,
+        video_output,
+        audio_expand,
+        audio_shrink,
+        video_expand,
+        video_shrink,
+    )
+    vmem = pl.BlockSpec(memory_space=pltpu.VMEM)
+    hbm = pl.BlockSpec(memory_space=pl.ANY)
+    streams = []
+    for extent in (video_width, audio_width) * 2:
+        streams += Stream.scratch(count, rows, extent)
+    bf16 = jnp.bfloat16
+    return pl.pallas_call(
+        functools.partial(block_kernel, count, video_width, audio_width),
+        out_shape=(
+            jax.ShapeDtypeStruct(video_state.shape, jnp.float32),
+            jax.ShapeDtypeStruct(audio_state.shape, jnp.float32),
+        ),
+        in_specs=[vmem] * 4 + [hbm] * len(weights),
+        out_specs=(vmem, vmem),
+        scratch_shapes=[pltpu.VMEM(weight.shape, weight.dtype) for weight in weights]
+        + streams
+        + [
+            pltpu.SemaphoreType.DMA((len(weights),)),
+            pltpu.VMEM((512, width), jnp.float32),
+            pltpu.VMEM((video_width, width), bf16),
+            pltpu.VMEM((video_width, width), bf16),
+            pltpu.VMEM((audio_width, width), bf16),
+            pltpu.VMEM((audio_width, width), bf16),
+            pltpu.VMEM((tokens, width), bf16),
+            pltpu.VMEM((tokens, width), bf16),
+            pltpu.VMEM((tokens, video_expand.shape[1]), bf16),
+            pltpu.VMEM((tokens, audio_expand.shape[1]), bf16),
+        ],
+        compiler_params=pltpu.CompilerParams(
+            collective_id=0, has_side_effects=True, vmem_limit_bytes=VMEM_BYTES
+        ),
+    )(video_state, audio_state, video_modulation, audio_modulation, *weights)
+
+
+def block(*arrays):
+    count = lax.axis_size("tensor")
+    rows = arrays[0].shape[0]
+    width = arrays[4].shape[1]
+    held = sum(array.size * array.dtype.itemsize for array in arrays[4:])
+    fits = held <= WEIGHT_BYTES and count * rows <= 64
+    shaped = count % 2 == 0 and 2 * rows % 8 == 0 and width % 128 == 0
+    tiled = all(extent % 512 == 0 for array in (arrays[0], arrays[1], arrays[10], arrays[12]) for extent in array.shape[1:])
+    return fused_block(*arrays) if fits and shaped and tiled else on_device(*arrays)
+
+
 def solution(mesh):
     placed = (
         P(("groups", "tensor"), None),
@@ -162,7 +568,7 @@
         P("tensor", None),
     )
     return jax.shard_map(
-        on_device,
+        block,
         mesh=mesh,
         in_specs=placed,
         out_specs=(P(("groups", "tensor"), None), P(("groups", "tensor"), None)),

time: 304 us -> 59 us (0.19)
  waiting for transfers between devices: 199 us -> 0 us
  Pallas kernels: 0 us -> 55.3 us
  blocking collectives: 45.4 us -> 0 us
  matrix products: 26.7 us -> 0 us
  between operations: 14.8 us -> 0.64 us
  other arithmetic: 12 us -> 0 us
    unnamed x4 -> x0, waiting for transfers between devices: 94.1 us -> none
    psum x1 -> x0, waiting for transfers between devices: 93.9 us -> none  [on_device(): full_term = lax.psum(partial_term, 'tensor')]
    pallas_call x0 -> x1, Pallas kernels: none -> 55.3 us  [fused_block(): pl.pallas_call(functools.partial(block_kernel, count, video_width, audio_...]
    all_gather x2 -> x0, blocking collectives: 45.4 us -> none  [the longest x1 24 us: on_device(): audio_normed = lax.all_gather(audio_own, 'tensor', axis=0, tiled=True)]
    dot_general x12 -> x0, matrix products: 26.7 us -> none  [the longest x2 13.4 us: feed_rows(): return jnp.dot(hidden, shrink, preferred_element_type=jnp.float32)]
    all_gather x1 -> x0, waiting for transfers between devices: 10.6 us -> none  [on_device(): video_whole = lax.all_gather(video_state, 'tensor', axis=0, tiled=True)]
    reduce_sum x8 -> x0, other arithmetic: 5.1 us -> none  [the longest x4 4.55 us: modulate(): jnp.mean(states * states, axis=-1, keepdims=True) + epsilon]
  transfers between devices with their start and end apart: 3 -> 0, of which waited for: 3 -> 0; matrix products, arithmetic and copies ran while one was open for 3% -> 0% of each run, Pallas kernels for 0% -> 0%
where the time goes in v1:
time: 59 us; the launch traced here: 58.8 us
  Pallas kernels  55.3 us (94%)
  local copies, waits for them, and re-layouts  2.85 us (5%)
  between operations  0.64 us (1%)
    pallas_call x1, Pallas kernels, fused_block(): pl.pallas_call(functools.partial(block_kernel, count, video_width, audio_...  55.3 us
    unnamed x2, local copies, waits for them, and re-layouts  2.85 us

profile of v1, /device:TPU:0, one launch (start us, length us, event | category | flops | bytes accessed | tf_op | source)
XLA Modules:
  0.0 58.8 jit_solution(4999936986569015134)
XLA Ops:
  0.6 55.3 %shard_map.149 = (f32[4,4096]{1,0:T(4,128)}, f32[4,2048]{1,0:T(4,128)}) custom-call(f32[4,4096]{1,0:T(4,128)} %refs_0_.1, f32[4,2048]{1,0:T(4,128)} %refs_1_.1, f32[6,4096]{1,0:T(8,128)} %refs_2_.1, f32[6,2048]{1,0:T(8,128)} %refs_3_.1, bf16[2048,128]{1,0:T(8,128)(2,1)} %refs_4_.1, bf16[4096,128]{1,0:T(8,128)(2,1)} %bitcast.3, bf16[4096,128]{1,0:T(8,128)(2,1)} %refs_6_.1, ...), custom_call_target="tpu_custom_call" | custom-call | tf_op jit(solution)/shard_map/pallas_call | solution.py:514
  55.9 1.5 %copy.18 = f32[4,4096]{1,0:T(4,128)} copy(f32[4,4096]{1,0:T(4,128)} %get-tuple-element.4) | data formatting | bytes 131072
  57.4 1.4 %copy.19 = f32[4,2048]{1,0:T(4,128)} copy(f32[4,2048]{1,0:T(4,128)} %get-tuple-element.5) | data formatting | bytes 65536

commit v2 on v1

--- a/solution.py
+++ b/solution.py
@@ -152,95 +152,115 @@
 WEIGHT_BYTES = 40 << 20
 
 
-def matmul_to(lhs_ref, weight_ref, tile, emit):
+def matmul_to(lhs_ref, weight_ref, first, extent, tile, emit):
     def body(i, carry):
-        columns = pl.ds(pl.multiple_of(i * tile, tile), tile)
-        emit(
-            columns,
-            jnp.dot(lhs_ref[...], weight_ref[:, columns], preferred_element_type=jnp.float32),
-        )
+        start = pl.multiple_of(i * tile, tile)
+        columns = pl.ds(pl.multiple_of(first + i * tile, tile), tile)
+        emit(start, jnp.dot(lhs_ref[...], weight_ref[:, columns], preferred_element_type=jnp.float32))
         return carry
 
-    lax.fori_loop(0, weight_ref.shape[1] // tile, body, 0)
+    lax.fori_loop(0, extent // tile, body, 0)
 
 
 class Stream:
-    names = ("own", "slots", "wide", "whole", "other", "paired", "sums", "terms", "total")
+    names = ("own", "slots", "wide", "other", "paired", "across", "crossed", "sums", "terms", "total")
 
     @staticmethod
     def scratch(count, rows, width):
-        chips = count // 2
+        chips, planes = count // 2, count // 4
         return [
             pltpu.VMEM((rows, width), jnp.bfloat16),
             pltpu.VMEM((count, rows, width), jnp.bfloat16),
             pltpu.VMEM((chips, 2 * rows, width), jnp.float32),
-            pltpu.VMEM((count * rows, width), jnp.bfloat16),
             pltpu.VMEM((chips, rows, width), jnp.bfloat16),
             pltpu.VMEM((chips, rows, width), jnp.bfloat16),
-            pltpu.VMEM((chips, rows, width), jnp.bfloat16),
-            pltpu.VMEM((chips, rows, width), jnp.bfloat16),
+            pltpu.VMEM((planes, rows, width), jnp.bfloat16),
+            pltpu.VMEM((planes, rows, width), jnp.bfloat16),
+            pltpu.VMEM((planes, rows, width), jnp.bfloat16),
+            pltpu.VMEM((planes, rows, width), jnp.bfloat16),
             pltpu.VMEM((rows, width), jnp.float32),
-            pltpu.SemaphoreType.DMA((2 * chips,)),
+            pltpu.SemaphoreType.DMA((chips,)),
+            pltpu.SemaphoreType.DMA((planes,)),
+            pltpu.SemaphoreType.DMA((planes,)),
             pltpu.SemaphoreType.DMA((count,)),
-            pltpu.SemaphoreType.DMA((chips + 1,)),
-            pltpu.SemaphoreType.DMA((chips + 1,)),
+            pltpu.SemaphoreType.DMA((planes + 2,)),
+            pltpu.SemaphoreType.DMA((planes + 2,)),
         ]
 
-    def __init__(self, refs, count):
+    def __init__(self, refs, whole, count):
         for name, ref in zip(self.names, refs):
             setattr(self, name, ref)
-        self.gather_send, self.gather_recv, self.scatter_send, self.scatter_recv = refs[len(self.names):]
-        self.count, self.chips = count, count // 2
+        (self.mate_send, self.side_send, self.plane_send, self.gather_recv, self.scatter_send,
+         self.scatter_recv) = refs[len(self.names):]
+        self.whole = whole
+        self.count, self.chips, self.planes = count, count // 2, count // 4
         self.rows = self.own.shape[0]
         self.me = lax.axis_index("tensor")
-        self.chip, self.core = self.me // 2, self.me % 2
-        self.mate = self.chip * 2 + (1 - self.core)
+        self.core, self.chip = self.me % 2, self.me // 2
+        self.side, self.plane = self.chip % 2, self.chip // 2
+        self.mate = self.at(self.plane, self.side, 1 - self.core)
+        self.beside = self.at(self.plane, 1 - self.side, self.core)
+
+    @staticmethod
+    def at(plane, side, core):
+        return (plane * 2 + side) * 2 + core
 
     def distant(self, step):
-        return lax.rem(self.chip + step, self.chips)
-
-    def to_mate(self, slot, source, send):
+        return lax.rem(self.plane + step, self.planes)
+
+    def send(self, slot, source, semaphore, goal):
         return pltpu.make_async_remote_copy(
             src_ref=source,
             dst_ref=self.slots.at[slot],
-            send_sem=self.gather_send.at[send],
+            send_sem=semaphore,
             recv_sem=self.gather_recv.at[slot],
-            device_id={"tensor": self.mate},
+            device_id={"tensor": goal},
             device_id_type=pl.DeviceIdType.MESH,
         )
 
-    def to_chip(self, step):
-        return pltpu.make_async_remote_copy(
-            src_ref=self.own,
-            dst_ref=self.slots.at[self.me],
-            send_sem=self.gather_send.at[step],
-            recv_sem=self.gather_recv.at[self.me],
-            device_id={"tensor": self.distant(step) * 2 + self.core},
-            device_id_type=pl.DeviceIdType.MESH,
-        )
+    def to_plane(self, step):
+        goal = self.at(self.distant(step), self.side, self.core)
+        return self.send(self.me, self.own, self.plane_send.at[step], goal)
+
+    def to_side(self, step):
+        slot = self.at(self.distant(step), self.side, self.core)
+        source = self.slots.at[slot] if step else self.own
+        return self.send(slot, source, self.side_send.at[step], self.beside)
+
+    def to_mate(self, step, side):
+        slot = self.at(self.distant(step), self.side if side == 0 else 1 - self.side, self.core)
+        source = self.slots.at[slot] if step or side else self.own
+        return self.send(slot, source, self.mate_send.at[2 * step + side], self.mate)
 
     def keep(self):
         return pltpu.make_async_copy(self.own, self.slots.at[self.me], self.gather_recv.at[self.me])
 
-    def gather_start(self):
-        for step in range(self.chips - 1, 0, -1):
-            self.to_chip(step).start()
-        self.to_mate(self.me, self.own, 0).start()
-        self.keep().start()
-
     def arrived(self, slot):
         pltpu.make_async_copy(self.slots.at[slot], self.slots.at[slot], self.gather_recv.at[slot]).wait()
 
-    def gather_forward(self):
-        for step in range(1, self.chips):
-            slot = self.distant(step) * 2 + self.core
-            self.arrived(slot)
-            self.to_mate(slot, self.slots.at[slot], self.chips + step).start()
+    def gather_start(self):
+        for step in range(1, self.planes):
+            self.to_plane(step).start()
+        self.to_side(0).start()
+        self.to_mate(0, 0).start()
+        self.keep().start()
+
+    def gather_planes(self):
+        for step in range(1, self.planes):
+            self.arrived(self.at(self.distant(step), self.side, self.core))
+            self.to_side(step).start()
+            self.to_mate(step, 0).start()
+
+    def gather_sides(self):
+        for step in range(self.planes):
+            self.arrived(self.at(self.distant(step), 1 - self.side, self.core))
+            self.to_mate(step, 1).start()
 
     def gather_finish(self):
         self.keep().wait()
-        for step in range(self.chips):
-            self.arrived(self.distant(step) * 2 + 1 - self.core)
+        for step in range(self.planes):
+            for side in range(2):
+                self.arrived(self.at(self.distant(step), side, 1 - self.core))
 
         def widen(chip, carry):
             self.wide[chip, : self.rows, :] = self.slots[2 * chip].astype(jnp.float32)
@@ -251,24 +271,35 @@
         self.whole[...] = self.wide[...].reshape(self.whole.shape).astype(jnp.bfloat16)
 
     def gather_drain(self):
-        for step in range(1, self.chips):
-            slot = self.distant(step) * 2 + self.core
-            self.to_chip(step).wait_send()
-            self.to_mate(slot, self.slots.at[slot], self.chips + step).wait_send()
-        self.to_mate(self.me, self.own, 0).wait_send()
-
-    def emit(self, columns, product):
-        self.wide[:, :, columns] = product.reshape(self.chips, 2 * self.rows, product.shape[1])
-
-    def swap(self):
+        for step in range(self.planes):
+            if step:
+                self.to_plane(step).wait_send()
+            self.to_side(step).wait_send()
+            for side in range(2):
+                self.to_mate(step, side).wait_send()
+
+    def emit(self, offset=0):
+        def keep(start, product):
+            columns = pl.ds(pl.multiple_of(start + offset, 128), product.shape[1])
+            self.wide[:, :, columns] = product.reshape(self.chips, 2 * self.rows, product.shape[1])
+
+        return keep
+
+    def trade(self, source, target, index, goal):
         return pltpu.make_async_remote_copy(
-            src_ref=self.other,
-            dst_ref=self.paired,
-            send_sem=self.scatter_send.at[self.chips],
-            recv_sem=self.scatter_recv.at[self.chips],
-            device_id={"tensor": self.mate},
+            src_ref=source,
+            dst_ref=target,
+            send_sem=self.scatter_send.at[index],
+            recv_sem=self.scatter_recv.at[index],
+            device_id={"tensor": goal},
             device_id_type=pl.DeviceIdType.MESH,
         )
+
+    def swap(self):
+        return self.trade(self.other, self.paired, self.planes, self.mate)
+
+    def cross(self):
+        return self.trade(self.across, self.crossed, self.planes + 1, self.beside)
 
     def halves(self, chip):
         rows = self.wide[chip]
@@ -276,6 +307,10 @@
         first = self.core == 0
         return jnp.where(first, low, high), jnp.where(first, high, low)
 
+    def of_pair(self, plane, side):
+        chip = plane * 2 + side
+        return self.halves(chip)[0] + self.paired[chip].astype(jnp.float32)
+
     def scatter_start(self):
         def body(chip, carry):
             self.other[chip] = self.halves(chip)[1].astype(jnp.bfloat16)
@@ -284,37 +319,49 @@
         lax.fori_loop(0, self.chips, body, 0)
         self.swap().start()
 
+    def scatter_sides(self):
+        self.swap().wait()
+
+        def body(plane, carry):
+            self.across[plane] = self.of_pair(plane, 1 - self.side).astype(jnp.bfloat16)
+            return carry
+
+        lax.fori_loop(0, self.planes, body, 0)
+        self.cross().start()
+
+    def of_column(self, plane):
+        return self.of_pair(plane, self.side) + self.crossed[plane].astype(jnp.float32)
+
     def term(self, step):
         goal = self.distant(step)
         return pltpu.make_async_remote_copy(
             src_ref=self.sums.at[goal],
-            dst_ref=self.terms.at[self.chip],
+            dst_ref=self.terms.at[self.plane],
             send_sem=self.scatter_send.at[step],
-            recv_sem=self.scatter_recv.at[self.chip],
-            device_id={"tensor": goal * 2 + self.core},
+            recv_sem=self.scatter_recv.at[self.plane],
+            device_id={"tensor": self.at(goal, self.side, self.core)},
             device_id_type=pl.DeviceIdType.MESH,
         )
 
-    def scatter_send_on(self):
-        self.swap().wait()
-        for step in range(1, self.chips):
+    def scatter_planes(self):
+        self.cross().wait()
+        for step in range(1, self.planes):
             goal = self.distant(step)
-            self.sums[goal] = (
-                self.halves(goal)[0] + self.paired[goal].astype(jnp.float32)
-            ).astype(jnp.bfloat16)
+            self.sums[goal] = self.of_column(goal).astype(jnp.bfloat16)
             self.term(step).start()
-        self.total[...] = self.halves(self.chip)[0] + self.paired[self.chip].astype(jnp.float32)
+        self.total[...] = self.of_column(self.plane)
 
     def scatter_finish(self):
-        for step in range(1, self.chips):
+        result = self.total[...]
+        for step in range(1, self.planes):
             source = self.distant(step)
             pltpu.make_async_copy(
                 self.terms.at[source], self.terms.at[source], self.scatter_recv.at[source]
             ).wait()
-            self.total[...] += self.terms[source].astype(jnp.float32)
-        for step in range(1, self.chips):
+            result += self.terms[source].astype(jnp.float32)
+        for step in range(1, self.planes):
             self.term(step).wait_send()
-        return self.total[...]
+        return result
 
 
 def split_pairs(pairs_ref, wide_ref, even_ref, odd_ref, rows):
@@ -365,22 +412,24 @@
     ).astype(jnp.bfloat16)
 
 
-def project(rows_ref, weight_ref):
-    return jnp.dot(rows_ref[...], weight_ref[...], preferred_element_type=jnp.float32).astype(jnp.bfloat16)
-
-
-def block_kernel(count, video_width, audio_width, *refs):
+def project(rows, weight):
+    return jnp.dot(rows, weight, preferred_element_type=jnp.float32)
+
+
+def block_kernel(count, *refs):
     video_state, audio_state, video_mod, audio_mod = refs[:4]
     weights_hbm = refs[4:14]
     video_out, audio_out = refs[14:16]
     weights = refs[16:26]
-    rest = refs[26:]
-    size = 13
-    video1, audio1, video2, audio2 = (
-        Stream(rest[i * size : (i + 1) * size], count) for i in range(4)
-    )
-    (weight_sem, pair_wide, video_key, video_value, audio_key, audio_value,
-     video_mixed, audio_mixed, video_hidden, audio_hidden) = rest[4 * size :]
+    (weight_sem, pair_wide, video_key, video_value, audio_key, audio_value, video_mixed, audio_mixed,
+     video_hidden, audio_hidden, video_sums, video_whole, audio_whole) = refs[26:39]
+    rest = refs[39:]
+    size = len(rest) // 6
+    half = video_state.shape[1] // 2
+    wholes = (audio_whole, video_whole.at[:, :half], video_whole.at[:, half:]) * 2
+    audio1, left1, right1, audio2, left2, right2 = (
+        Stream(rest[i * size : (i + 1) * size], wholes[i], count) for i in range(6)
+    )
     loads = [
         pltpu.make_async_copy(hbm, vmem, weight_sem.at[i])
         for i, (hbm, vmem) in enumerate(zip(weights_hbm, weights))
@@ -391,85 +440,131 @@
         load.start()
 
     barrier = pltpu.get_barrier_semaphore()
-    for step in range(1, video1.chips):
+    friends = [audio1.at(audio1.distant(step), audio1.side, audio1.core) for step in range(1, audio1.planes)]
+    friends += [audio1.mate, audio1.beside]
+    for friend in friends:
         pl.semaphore_signal(
-            barrier,
-            inc=1,
-            device_id={"tensor": video1.distant(step) * 2 + video1.core},
-            device_id_type=pl.DeviceIdType.MESH,
+            barrier, inc=1, device_id={"tensor": friend}, device_id_type=pl.DeviceIdType.MESH
         )
-    pl.semaphore_signal(
-        barrier, inc=1, device_id={"tensor": video1.mate}, device_id_type=pl.DeviceIdType.MESH
-    )
     audio1.own[...] = modulate_rows(audio_state[...], audio_mod, 0)
-    video1.own[...] = modulate_rows(video_state[...], video_mod, 0)
-    pl.semaphore_wait(barrier, video1.chips)
+    video_own = modulate_rows(video_state[...], video_mod, 0)
+    left1.own[...] = video_own[:, :half]
+    right1.own[...] = video_own[:, half:]
+    pl.semaphore_wait(barrier, len(friends))
 
     audio1.gather_start()
-    video1.gather_start()
+    left1.gather_start()
+    right1.gather_start()
     loads[1].wait()
     split_pairs(audio_pairs, pair_wide, audio_key, audio_value, pair_wide.shape[0] // 2)
-    audio1.gather_forward()
+    audio1.gather_planes()
     loads[3].wait()
     split_pairs(video_pairs, pair_wide, video_key, video_value, pair_wide.shape[0] // 2)
+    audio1.gather_sides()
+    left1.gather_planes()
     audio1.gather_finish()
     loads[0].wait()
-    audio_queries = project(audio1.whole, audio_query)
-    audio_keys = project(audio1.whole, audio_key)
-    audio_values = project(audio1.whole, audio_value)
-    video1.gather_forward()
-    video1.gather_finish()
+    bf16 = jnp.bfloat16
+    audio_queries = project(audio_whole[...], audio_query[...]).astype(bf16)
+    left1.gather_sides()
+    right1.gather_planes()
+    audio_keys = project(audio_whole[...], audio_key[...]).astype(bf16)
+    audio_values = project(audio_whole[...], audio_value[...]).astype(bf16)
+    left1.gather_finish()
     loads[2].wait()
-    video_keys = project(video1.whole, video_key)
-    video_values = project(video1.whole, video_value)
+    rows = left1.whole[...]
+    video_keys = project(rows, video_key[:half, :])
+    right1.gather_sides()
+    video_values = project(rows, video_value[:half, :])
+    video_queries = project(rows, video_query[:half, :])
+    right1.gather_finish()
+    rows = right1.whole[...]
+    video_keys = (video_keys + project(rows, video_key[half:, :])).astype(bf16)
+    video_values = (video_values + project(rows, video_value[half:, :])).astype(bf16)
+    video_queries = (video_queries + project(rows, video_query[half:, :])).astype(bf16)
+    video_mixed[...] = attend(video_queries, audio_keys, audio_values)
+    loads[5].wait()
+    matmul_to(video_mixed, video_output, 0, half, 512, left1.emit())
+    left1.scatter_start()
+    matmul_to(video_mixed, video_output, half, half, 512, right1.emit())
+    right1.scatter_start()
+    left1.scatter_sides()
     audio_mixed[...] = attend(audio_queries, video_keys, video_values)
+    right1.scatter_sides()
     loads[4].wait()
-    matmul_to(audio_mixed, audio_output, 512, audio1.emit)
+    matmul_to(audio_mixed, audio_output, 0, audio_output.shape[1], 512, audio1.emit())
     audio1.scatter_start()
-    video_queries = project(video1.whole, video_query)
-    video_mixed[...] = attend(video_queries, audio_keys, audio_values)
-    audio1.scatter_send_on()
-    loads[5].wait()
-    matmul_to(video_mixed, video_output, 512, video1.emit)
-    video1.scatter_start()
+    left1.scatter_planes()
+    audio1.scatter_sides()
+    right1.scatter_planes()
     audio1.gather_drain()
-    video1.gather_drain()
-    video1.scatter_send_on()
+    left1.gather_drain()
+    right1.gather_drain()
+    audio1.scatter_planes()
+    video_mid = video_state[...] + video_mod[2:3, :] * jnp.concatenate(
+        [left1.scatter_finish(), right1.scatter_finish()], axis=1
+    )
+    video_out[...] = video_mid
+    video_own = modulate_rows(video_mid, video_mod, 3)
+    left2.own[...] = video_own[:, :half]
+    right2.own[...] = video_own[:, half:]
+    left2.gather_start()
+    right2.gather_start()
     audio_mid = audio_state[...] + audio_mod[2:3, :] * audio1.scatter_finish()
     audio_out[...] = audio_mid
     audio2.own[...] = modulate_rows(audio_mid, audio_mod, 3)
     audio2.gather_start()
-    video_mid = video_state[...] + video_mod[2:3, :] * video1.scatter_finish()
-    video_out[...] = video_mid
-    video2.own[...] = modulate_rows(video_mid, video_mod, 3)
-    video2.gather_start()
-    audio2.gather_forward()
+    left2.gather_planes()
+    right2.gather_planes()
+    left2.gather_sides()
+    audio2.gather_planes()
+    left2.gather_finish()
+    loads[8].wait()
+    hidden_width = video_hidden.shape[1]
+
+    def keep_sums(start, product):
+        video_sums[:, pl.ds(start, product.shape[1])] = product
+
+    def keep_video(start, product):
+        columns = pl.ds(start, product.shape[1])
+        video_hidden[:, columns] = jax.nn.gelu(video_sums[:, columns] + product, approximate=True).astype(bf16)
+
+    def keep_audio(start, product):
+        audio_hidden[:, pl.ds(start, product.shape[1])] = jax.nn.gelu(product, approximate=True).astype(bf16)
+
+    right2.gather_sides()
+    matmul_to(left2.whole, video_expand.at[:half, :], 0, hidden_width, 256, keep_sums)
+    audio2.gather_sides()
+    right2.gather_finish()
+    matmul_to(right2.whole, video_expand.at[half:, :], 0, hidden_width, 256, keep_video)
+    loads[9].wait()
+    matmul_to(video_hidden, video_shrink, 0, half, 512, left2.emit())
+    left2.scatter_start()
+    matmul_to(video_hidden, video_shrink, half, half, 512, right2.emit())
+    right2.scatter_start()
+    left2.scatter_sides()
     audio2.gather_finish()
-
-    def keep_hidden(target):
-        def emit(columns, product):
-            target[:, columns] = jax.nn.gelu(product, approximate=True).astype(jnp.bfloat16)
-
-        return emit
-
     loads[6].wait()
-    matmul_to(audio2.whole, audio_expand, 256, keep_hidden(audio_hidden))
+    matmul_to(audio2.whole, audio_expand, 0, audio_hidden.shape[1], 256, keep_audio)
+    right2.scatter_sides()
     loads[7].wait()
-    matmul_to(audio_hidden, audio_shrink, 512, audio2.emit)
+    matmul_to(audio_hidden, audio_shrink, 0, audio_shrink.shape[1], 512, audio2.emit())
     audio2.scatter_start()
-    video2.gather_forward()
-    audio2.scatter_send_on()
-    video2.gather_finish()
-    loads[8].wait()
-    matmul_to(video2.whole, video_expand, 256, keep_hidden(video_hidden))
-    loads[9].wait()
-    matmul_to(video_hidden, video_shrink, 512, video2.emit)
-    video2.scatter_start()
+    left2.scatter_planes()
+    audio2.scatter_sides()
+    right2.scatter_planes()
+    audio2.gather_drain()
+    left2.gather_drain()
+    right2.gather_drain()
+    audio2.scatter_planes()
+    video_out[:, :half] += video_mod[5:6, :half] * left2.scatter_finish()
+    video_out[:, half:] += video_mod[5:6, half:] * right2.scatter_finish()
     audio_out[...] += audio_mod[5:6, :] * audio2.scatter_finish()
-    audio2.gather_drain()
-    video2.gather_drain()
-    video2.scatter_send_on()
-    video_out[...] += video_mod[5:6, :] * video2.scatter_finish()
+
+
+def hand_over(video_ref, audio_ref, video_out, audio_out):
+    video_out[...] = video_ref[...]
+    audio_out[...] = audio_ref[...]
 
 
 def fused_block(
@@ -508,19 +603,19 @@
     vmem = pl.BlockSpec(memory_space=pltpu.VMEM)
     hbm = pl.BlockSpec(memory_space=pl.ANY)
     streams = []
-    for extent in (video_width, audio_width) * 2:
+    for extent in (audio_width, video_width // 2, video_width // 2) * 2:
         streams += Stream.scratch(count, rows, extent)
     bf16 = jnp.bfloat16
-    return pl.pallas_call(
-        functools.partial(block_kernel, count, video_width, audio_width),
-        out_shape=(
-            jax.ShapeDtypeStruct(video_state.shape, jnp.float32),
-            jax.ShapeDtypeStruct(audio_state.shape, jnp.float32),
-        ),
+    results = (
+        jax.ShapeDtypeStruct(video_state.shape, jnp.float32),
+        jax.ShapeDtypeStruct(audio_state.shape, jnp.float32),
+    )
+    video_next, audio_next = pl.pallas_call(
+        functools.partial(block_kernel, count),
+        out_shape=results,
         in_specs=[vmem] * 4 + [hbm] * len(weights),
         out_specs=(vmem, vmem),
         scratch_shapes=[pltpu.VMEM(weight.shape, weight.dtype) for weight in weights]
-        + streams
         + [
             pltpu.SemaphoreType.DMA((len(weights),)),
             pltpu.VMEM((512, width), jnp.float32),
@@ -532,11 +627,18 @@
             pltpu.VMEM((tokens, width), bf16),
             pltpu.VMEM((tokens, video_expand.shape[1]), bf16),
             pltpu.VMEM((tokens, audio_expand.shape[1]), bf16),
-        ],
+            pltpu.VMEM((tokens, video_expand.shape[1]), jnp.float32),
+            pltpu.VMEM((tokens, video_width), bf16),
+            pltpu.VMEM((tokens, audio_width), bf16),
+        ]
+        + streams,
         compiler_params=pltpu.CompilerParams(
             collective_id=0, has_side_effects=True, vmem_limit_bytes=VMEM_BYTES
         ),
     )(video_state, audio_state, video_modulation, audio_modulation, *weights)
+    return pl.pallas_call(
+        hand_over, out_shape=results, in_specs=[vmem] * 2, out_specs=(vmem, vmem)
+    )(video_next, audio_next)
 
 
 def block(*arrays):
@@ -545,8 +647,10 @@
     width = arrays[4].shape[1]
     held = sum(array.size * array.dtype.itemsize for array in arrays[4:])
     fits = held <= WEIGHT_BYTES and count * rows <= 64
-    shaped = count % 2 == 0 and 2 * rows % 8 == 0 and width % 128 == 0
-    tiled = all(extent % 512 == 0 for array in (arrays[0], arrays[1], arrays[10], arrays[12]) for extent in array.shape[1:])
+    shaped = count % 4 == 0 and 2 * rows % 8 == 0 and width % 128 == 0
+    tiled = all(array.shape[1] % 1024 == 0 for array in arrays[:2]) and all(
+        arrays[i].shape[1] % 256 == 0 for i in (10, 12)
+    )
     return fused_block(*arrays) if fits and shaped and tiled else on_device(*arrays)
 
 

time: 59 us -> 63.3 us (1.073)
  Pallas kernels: 55.3 us -> 62.5 us
  local copies, waits for them, and re-layouts: 2.85 us -> 0 us
    pallas_call x1 -> x2, Pallas kernels: 55.3 us -> 62.5 us  [the longest x1 61 us: fused_block(): pl.pallas_call(functools.partial(block_kernel, count), out_shape=results,...]
    unnamed x2 -> x0, local copies, waits for them, and re-layouts: 2.85 us -> none
where the time goes in v2:
time: 63.3 us; the launch traced here: 63.2 us
  Pallas kernels  62.5 us (99%)
  between operations  0.64 us (1%)
    pallas_call x1, Pallas kernels, fused_block(): pl.pallas_call(functools.partial(block_kernel, count), out_shape=results,...  61 us
    pallas_call x1, Pallas kernels, fused_block(): pl.pallas_call(hand_over, out_shape=results, in_specs=[vmem] * 2, out_spe...  1.48 us

profile of v2, /device:TPU:0, one launch (start us, length us, event | category | flops | bytes accessed | tf_op | source)
XLA Modules:
  0.0 63.2 jit_solution(2961071732514970709)
XLA Ops:
  0.6 61.0 %shard_map.149 = (f32[4,4096]{1,0:T(4,128)}, f32[4,2048]{1,0:T(4,128)}) custom-call(f32[4,4096]{1,0:T(4,128)} %refs_0_.1, f32[4,2048]{1,0:T(4,128)} %refs_1_.1, f32[6,4096]{1,0:T(8,128)} %refs_2_.1, f32[6,2048]{1,0:T(8,128)} %refs_3_.1, bf16[2048,128]{1,0:T(8,128)(2,1)} %refs_4_.1, bf16[4096,128]{1,0:T(8,128)(2,1)} %bitcast.3, bf16[4096,128]{1,0:T(8,128)(2,1)} %refs_6_.1, ...), custom_call_target="tpu_custom_call" | custom-call | tf_op jit(solution)/shard_map/pallas_call | solution.py:613
  61.7 1.5 %shard_map.150 = (f32[4,4096]{1,0:T(4,128)}, f32[4,2048]{1,0:T(4,128)}) custom-call(f32[4,4096]{1,0:T(4,128)} %get-tuple-element.4.video_ref, f32[4,2048]{1,0:T(4,128)} %get-tuple-element.5.audio_ref), custom_call_target="tpu_custom_call" | custom-call | tf_op jit(solution)/shard_map/pallas_call | solution.py:639

commit v3 on v1

--- a/solution.py
+++ b/solution.py
@@ -472,6 +472,11 @@
     video_out[...] += video_mod[5:6, :] * video2.scatter_finish()
 
 
+def hand_over(video_ref, audio_ref, video_out, audio_out):
+    video_out[...] = video_ref[...]
+    audio_out[...] = audio_ref[...]
+
+
 def fused_block(
     video_state,
     audio_state,
@@ -511,12 +516,13 @@
     for extent in (video_width, audio_width) * 2:
         streams += Stream.scratch(count, rows, extent)
     bf16 = jnp.bfloat16
-    return pl.pallas_call(
+    results = (
+        jax.ShapeDtypeStruct(video_state.shape, jnp.float32),
+        jax.ShapeDtypeStruct(audio_state.shape, jnp.float32),
+    )
+    video_next, audio_next = pl.pallas_call(
         functools.partial(block_kernel, count, video_width, audio_width),
-        out_shape=(
-            jax.ShapeDtypeStruct(video_state.shape, jnp.float32),
-            jax.ShapeDtypeStruct(audio_state.shape, jnp.float32),
-        ),
+        out_shape=results,
         in_specs=[vmem] * 4 + [hbm] * len(weights),
         out_specs=(vmem, vmem),
         scratch_shapes=[pltpu.VMEM(weight.shape, weight.dtype) for weight in weights]
@@ -537,6 +543,9 @@
             collective_id=0, has_side_effects=True, vmem_limit_bytes=VMEM_BYTES
         ),
     )(video_state, audio_state, video_modulation, audio_modulation, *weights)
+    return pl.pallas_call(
+        hand_over, out_shape=results, in_specs=[vmem] * 2, out_specs=(vmem, vmem)
+    )(video_next, audio_next)
 
 
 def block(*arrays):
@@ -546,7 +555,9 @@
     held = sum(array.size * array.dtype.itemsize for array in arrays[4:])
     fits = held <= WEIGHT_BYTES and count * rows <= 64
     shaped = count % 2 == 0 and 2 * rows % 8 == 0 and width % 128 == 0
-    tiled = all(extent % 512 == 0 for array in (arrays[0], arrays[1], arrays[10], arrays[12]) for extent in array.shape[1:])
+    tiled = all(array.shape[1] % 512 == 0 for array in arrays[:2]) and all(
+        arrays[i].shape[1] % 256 == 0 for i in (10, 12)
+    )
     return fused_block(*arrays) if fits and shaped and tiled else on_device(*arrays)
 
 

time: 59 us -> 57.6 us (0.976)
  local copies, waits for them, and re-layouts: 2.85 us -> 0 us
  Pallas kernels: 55.3 us -> 56.7 us
    unnamed x2 -> x0, local copies, waits for them, and re-layouts: 2.85 us -> none
    pallas_call x0 -> x1, Pallas kernels: none -> 1.48 us  [fused_block(): pl.pallas_call(hand_over, out_shape=results, in_specs=[vmem] * 2, out_spe...]
where the time goes in v3:
time: 57.6 us; the launch traced here: 57.4 us
  Pallas kernels  56.7 us (98%)
  between operations  0.64 us (1%)
    pallas_call x1, Pallas kernels, fused_block(): pl.pallas_call(functools.partial(block_kernel, count, video_width, audio_...  55.3 us
    pallas_call x1, Pallas kernels, fused_block(): pl.pallas_call(hand_over, out_shape=results, in_specs=[vmem] * 2, out_spe...  1.48 us

profile of v3, /device:TPU:0, one launch (start us, length us, event | category | flops | bytes accessed | tf_op | source)
XLA Modules:
  0.0 57.4 jit_solution(11447819096393459412)
XLA Ops:
  0.6 55.3 %shard_map.149 = (f32[4,4096]{1,0:T(4,128)}, f32[4,2048]{1,0:T(4,128)}) custom-call(f32[4,4096]{1,0:T(4,128)} %refs_0_.1, f32[4,2048]{1,0:T(4,128)} %refs_1_.1, f32[6,4096]{1,0:T(8,128)} %refs_2_.1, f32[6,2048]{1,0:T(8,128)} %refs_3_.1, bf16[2048,128]{1,0:T(8,128)(2,1)} %refs_4_.1, bf16[4096,128]{1,0:T(8,128)(2,1)} %bitcast.3, bf16[4096,128]{1,0:T(8,128)(2,1)} %refs_6_.1, ...), custom_call_target="tpu_custom_call" | custom-call | tf_op jit(solution)/shard_map/pallas_call | solution.py:523
  55.9 1.5 %shard_map.150 = (f32[4,4096]{1,0:T(4,128)}, f32[4,2048]{1,0:T(4,128)}) custom-call(f32[4,4096]{1,0:T(4,128)} %get-tuple-element.4.video_ref, f32[4,2048]{1,0:T(4,128)} %get-tuple-element.5.audio_ref), custom_call_target="tpu_custom_call" | custom-call | tf_op jit(solution)/shard_map/pallas_call | solution.py:546
